TPU v7x, 256 devices: a whole 4x4x8 slice. The times are simulated.
256 devices in a mesh: px: 4 (over y), py: 8 (over z), fr: 8 (over x, core).
Axes of the slice: x: 4, y: 4, z: 8, core: 2. Of those that a mesh axis runs over, the one named last changes fastest.
Arguments:
- frames: bfloat16 [32, 2048, 2048], P('fr', 'px', 'py'), may hold values from 0.019897461 to 1
- a_start: float32 [64, 2048], P(None, 'px'), may hold values from 0.1 to 1
- b_start: float32 [64, 2048], P(None, 'py'), may hold values from 0.1 to 10, as said below
- c_start: float32 [64, 32], P(None, 'fr'), may hold values from 0.1 to 10, as said below
Outputs:
- a_factor: float32 [64, 2048], P(None, 'px')
- b_factor: float32 [64, 2048], P(None, 'py')
- c_factor: float32 [64, 32], P(None, 'fr')
Inputs may be any that keep to these rules, and one draw needn't show every extreme that they name: `b_start`: entries are positive. `c_start`: entries are positive.
All inputs are finite; a program needn't handle non-finite values.
Results may differ from a plain program's by a relative error of at most 0.0003.
Values sent between devices are 32-bit elements; how exact they have to be, the bound alone decides.
A program may use at most 64 MiB of HBM per device.

v0:
```python
import functools

import jax
import jax.numpy as jnp
from jax import lax
from jax.experimental import pallas as pl
from jax.experimental.pallas import tpu as pltpu
from jax.sharding import PartitionSpec as P

PASSES = 4
HI = lax.Precision.HIGHEST
F32 = jnp.float32
BF16 = jnp.bfloat16


def nt(x, y):
    return lax.dot_general(x, y, (((1,), (1,)), ((), ())), precision=HI, preferred_element_type=F32)


class Group:
    def __init__(self, axis, size):
        self.axis, self.size, self.me = axis, size, lax.axis_index(axis)
        half = size // 2
        self.offsets = sorted(range(1, size), key=lambda d: -min(d, size - d))

    def peer(self, d):
        return lax.rem(self.me + d, self.size)

    def source(self, d):
        return lax.rem(self.me + self.size - d, self.size)

    def copy(self, src, dst, sems, d):
        return pltpu.make_async_remote_copy(
            src_ref=src,
            dst_ref=dst,
            send_sem=sems.at[0, d],
            recv_sem=sems.at[1, d],
            device_id={self.axis: self.peer(d)},
            device_id_type=pl.DeviceIdType.MESH,
        )

    def start(self, src_for, dst, sems):
        copies = [self.copy(src_for(self.peer(d)), dst(self.me), sems, d) for d in self.offsets]
        for c in copies:
            c.start()
        return copies

    def arrive(self, dst, sems):
        for d in reversed(self.offsets):
            slot = dst(self.source(d))
            self.copy(slot, slot, sems, d).wait_recv()


def kernel(
    sizes,
    frames,
    a_start,
    b_start,
    c_start,
    a_out,
    b_out,
    c_out,
    a_buf,
    b_buf,
    local_a,
    local_b,
    shared,
    ra,
    za,
    rb,
    yb,
    yc,
    zc,
    cg,
    ga,
    gb,
    h_ref,
    s_ra,
    s_za,
    s_ga,
    s_rb,
    s_yb,
    s_gb,
    s_yc,
    s_zc,
    s_cg,
    s_aa,
    s_ab,
):
    npx, npy, nfr = sizes
    ys, zs, fs = Group("px", npx), Group("py", npy), Group("fr", nfr)
    groups = (ys, zs, fs)
    rank, i_len = a_start.shape
    j_len = b_start.shape[1]
    kk = c_start.shape[1]
    rows = rank // nfr
    own = pl.ds(pl.multiple_of(fs.me * rows, rows), rows)

    def block(f):
        return pl.ds(pl.multiple_of(f * rows, rows), rows)

    barrier = pltpu.get_barrier_semaphore()
    for g in groups:
        for d in g.offsets:
            pl.semaphore_signal(
                barrier, inc=1, device_id={g.axis: g.peer(d)}, device_id_type=pl.DeviceIdType.MESH
            )

    eye = lax.broadcasted_iota(jnp.int32, (rank, rank), 0) == lax.broadcasted_iota(
        jnp.int32, (rank, rank), 1
    )
    live = (lax.broadcasted_iota(jnp.int32, (8, 128), 0) < kk) & (
        lax.broadcasted_iota(jnp.int32, (8, 128), 1) < rank
    )

    def tile_of(columns):
        turned = [jnp.sum(jnp.where(eye, c, 0.0), axis=0, keepdims=True) for c in columns]
        low = jnp.concatenate(turned + [jnp.zeros((8 - kk, rank), F32)], axis=0)
        return jnp.concatenate([low, jnp.zeros((8, 128 - rank), F32)], axis=1)

    def columns_of(tile):
        return [
            jnp.sum(jnp.where(eye, tile[k : k + 1, :rank], 0.0), axis=1, keepdims=True)
            for k in range(kk)
        ]

    def packed(gram):
        return jnp.concatenate([gram[: rank // 2], gram[rank // 2 :]], axis=1)

    def unpacked(pack):
        return jnp.concatenate([pack[:, :rank], pack[:, rank:]], axis=0)

    def total(ref, n):
        out = ref[0]
        for s in range(1, n):
            out = out + ref[s]
        return out

    def make_local_a(b, c_cols):
        b_half = b.astype(BF16)
        out = None
        for k in range(kk):
            part = lax.dot_general(
                b_half, frames[k], (((1,), (1,)), ((), ())), preferred_element_type=F32
            )
            out = c_cols[k] * part if out is None else out + c_cols[k] * part
        local_a[...] = out

    a_buf[0] = a_start[...]
    b_buf[0] = b_start[...]
    c_cols = [c_start[:, k : k + 1] for k in range(kk)]
    cg[fs.me] = tile_of(c_cols)
    gb[zs.me] = packed(nt(b_start[...], b_start[...]))

    pl.semaphore_wait(barrier, sum(g.size - 1 for g in groups))
    pending = []
    pending += zs.start(lambda p: gb.at[zs.me], lambda s: gb.at[s], s_gb)
    pending += fs.start(lambda p: cg.at[fs.me], lambda s: cg.at[s], s_cg)

    def flush(pending):
        for c in pending:
            c.wait_send()
        pending.clear()

    gram_b = None
    for step in range(PASSES):
        now, new = step % 2, (step + 1) % 2
        make_local_a(b_buf[now], c_cols)
        sent = fs.start(lambda p: local_a.at[block(p)], lambda s: ra.at[s], s_ra)
        fs.arrive(lambda s: cg.at[s], s_cg)
        if gram_b is None:
            zs.arrive(lambda s: gb.at[s], s_gb)
            gram_b = unpacked(total(gb, npy))
        every_c = cg[...].reshape(nfr * 8, 128)
        gram_c = lax.dot_general(
            every_c, every_c, (((0,), (0,)), ((), ())), precision=HI, preferred_element_type=F32
        )[:rank, :rank]
        h_ref[...] = gram_b * gram_c
        lower = jnp.dot(h_ref[own, :], a_buf[now], precision=HI, preferred_element_type=F32)
        scale = a_buf[now, own, :]
        flush(pending)
        ra[fs.me] = local_a[own, :]
        fs.arrive(lambda s: ra.at[s], s_ra)
        za[zs.me] = total(ra, nfr)
        pending += sent
        sent = zs.start(lambda p: za.at[zs.me], lambda s: za.at[s], s_za)
        flush(pending)
        zs.arrive(lambda s: za.at[s], s_za)
        a_buf[new, own, :] = scale * total(za, npy) / lower
        pending += sent
        sent = fs.start(
            lambda p: a_buf.at[new, own, :], lambda s: a_buf.at[new, block(s), :], s_aa
        )
        flush(pending)
        fs.arrive(lambda s: a_buf.at[new, block(s), :], s_aa)
        pending += sent

        a_half = a_buf[new].astype(BF16)
        out = None
        for k in range(kk):
            part = jnp.dot(a_half, frames[k], preferred_element_type=F32)
            shared[k] = part
            out = c_cols[k] * part if out is None else out + c_cols[k] * part
        local_b[...] = out
        sent = fs.start(lambda p: local_b.at[block(p)], lambda s: rb.at[s], s_rb)
        ga[ys.me] = packed(nt(a_buf[new], a_buf[new]))
        sent += ys.start(lambda p: ga.at[ys.me], lambda s: ga.at[s], s_ga)
        rb[fs.me] = local_b[own, :]
        flush(pending)
        fs.arrive(lambda s: rb.at[s], s_rb)
        yb[ys.me] = total(rb, nfr)
        pending += sent
        sent = ys.start(lambda p: yb.at[ys.me], lambda s: yb.at[s], s_yb)
        ys.arrive(lambda s: ga.at[s], s_ga)
        gram_a = unpacked(total(ga, npx))
        h_ref[...] = gram_a * gram_c
        lower = jnp.dot(h_ref[own, :], b_buf[now], precision=HI, preferred_element_type=F32)
        scale = b_buf[now, own, :]
        flush(pending)
        ys.arrive(lambda s: yb.at[s], s_yb)
        b_buf[new, own, :] = scale * total(yb, npx) / lower
        pending += sent
        sent = fs.start(
            lambda p: b_buf.at[new, own, :], lambda s: b_buf.at[new, block(s), :], s_ab
        )
        flush(pending)
        fs.arrive(lambda s: b_buf.at[new, block(s), :], s_ab)
        pending += sent

        b_new = b_buf[new]
        yc[ys.me] = tile_of(
            [jnp.sum(shared[k] * b_new, axis=1, keepdims=True) for k in range(kk)]
        )
        sent = ys.start(lambda p: yc.at[ys.me], lambda s: yc.at[s], s_yc)
        gb[zs.me] = packed(nt(b_new, b_new))
        sent += zs.start(lambda p: gb.at[zs.me], lambda s: gb.at[s], s_gb)
        flush(pending)
        ys.arrive(lambda s: yc.at[s], s_yc)
        zc[zs.me] = total(yc, npx)
        pending += sent
        sent = zs.start(lambda p: zc.at[zs.me], lambda s: zc.at[s], s_zc)
        zs.arrive(lambda s: gb.at[s], s_gb)
        gram_b = unpacked(total(gb, npy))
        c_tile = cg[fs.me]
        lower = jnp.dot(
            c_tile[:, :rank], gram_a * gram_b, precision=HI, preferred_element_type=F32
        )
        lower = jnp.concatenate([lower, jnp.ones((8, 128 - rank), F32)], axis=1)
        flush(pending)
        zs.arrive(lambda s: zc.at[s], s_zc)
        c_tile = jnp.where(live, c_tile * total(zc, npy) / jnp.where(live, lower, 1.0), 0.0)
        c_cols = columns_of(c_tile)
        pending += sent
        if step + 1 < PASSES:
            cg[fs.me] = c_tile
            pending += fs.start(lambda p: cg.at[fs.me], lambda s: cg.at[s], s_cg)
    flush(pending)
    a_out[...] = a_buf[PASSES % 2]
    b_out[...] = b_buf[PASSES % 2]
    c_out[...] = jnp.concatenate(c_cols, axis=1)


def body(sizes, frames, a_start, b_start, c_start):
    npx, npy, nfr = sizes
    rank, i_len = a_start.shape
    j_len = b_start.shape[1]
    kk = c_start.shape[1]
    rows = rank // nfr
    vmem = pl.BlockSpec(memory_space=pltpu.VMEM)

    def sems(n):
        return pltpu.SemaphoreType.DMA((2, n))

    return pl.pallas_call(
        functools.partial(kernel, sizes),
        name="cp",
        out_shape=[
            jax.ShapeDtypeStruct((rank, i_len), F32),
            jax.ShapeDtypeStruct((rank, j_len), F32),
            jax.ShapeDtypeStruct((rank, kk), F32),
        ],
        in_specs=[vmem] * 4,
        out_specs=[vmem] * 3,
        scratch_shapes=[
            pltpu.VMEM((2, rank, i_len), F32),
            pltpu.VMEM((2, rank, j_len), F32),
            pltpu.VMEM((rank, i_len), F32),
            pltpu.VMEM((rank, j_len), F32),
            pltpu.VMEM((kk, rank, j_len), F32),
            pltpu.VMEM((nfr, rows, i_len), F32),
            pltpu.VMEM((npy, rows, i_len), F32),
            pltpu.VMEM((nfr, rows, j_len), F32),
            pltpu.VMEM((npx, rows, j_len), F32),
            pltpu.VMEM((npx, 8, 128), F32),
            pltpu.VMEM((npy, 8, 128), F32),
            pltpu.VMEM((nfr, 8, 128), F32),
            pltpu.VMEM((npx, rank // 2, 2 * rank), F32),
            pltpu.VMEM((npy, rank // 2, 2 * rank), F32),
            pltpu.VMEM((rank, rank), F32),
            sems(nfr),
            sems(npy),
            sems(npx),
            sems(nfr),
            sems(npx),
            sems(npy),
            sems(npx),
            sems(npy),
            sems(nfr),
            sems(nfr),
            sems(nfr),
        ],
        compiler_params=pltpu.CompilerParams(collective_id=0, has_side_effects=True),
    )(frames, a_start, b_start, c_start)


def solution(mesh):
    sizes = (mesh.shape["px"], mesh.shape["py"], mesh.shape["fr"])
    return jax.shard_map(
        functools.partial(body, sizes),
        mesh=mesh,
        in_specs=(P("fr", "px", "py"), P(None, "px"), P(None, "py"), P(None, "fr")),
        out_specs=(P(None, "px"), P(None, "py"), P(None, "fr")),
        check_vma=False,
    )
```

profile of v0, /device:TPU:1, one launch (start us, length us, event | category | flops | bytes accessed | tf_op | source)
XLA Modules:
  0.0 147.8 jit_solution(13952461893089829873)
XLA Ops:
  0.6 1.4 copy.7.c_start
  2.0 142.1 %cp.1 = (f32[64,512]{1,0:T(8,128)}, f32[64,256]{1,0:T(8,128)}, f32[64,4]{1,0:T(8,128)}) custom-call(bf16[4,512,256]{2,1,0:T(8,128)(2,1)} %frames.1, f32[64,512]{1,0:T(8,128)} %a_start.1, f32[64,256]{1,0:T(8,128)} %b_start.1, f32[64,4]{1,0:T(8,128)} %copy.7.c_start), custom_call_target="tpu_custom_call" | custom-call | tf_op jit(solution)/shard_map/cp/pallas_call | solution.py:274
  144.2 1.4 copy.8
  145.6 0.0 copy-start
  145.6 1.6 %copy.11 = f32[64,512]{1,0:T(8,128)} copy(f32[64,512]{1,0:T(8,128)} %get-tuple-element.9) | data formatting | bytes 262144
  147.2 0.0 copy-done
  147.2 0.6 copy.12
Async XLA Ops:
  145.6 1.6 %copy-start = (f32[64,256]{1,0:T(8,128)S(1)}, f32[64,256]{1,0:T(8,128)}, u32[]{:S(2)}) copy-start(f32[64,256]{1,0:T(8,128)} %get-tuple-element.10) | copy-start | bytes 196612
where the time goes:
time: 148 us
  Pallas kernels  142 us (96%)
  local copies, waits for them, and re-layouts  5.03 us (3%)
    pallas_call x1, Pallas kernels, body(): pl.pallas_call(functools.partial(kernel, sizes), name='cp', out_shape=[ja...  142 us
    unnamed x5, local copies, waits for them, and re-layouts  3.62 us

commit v1 on v0

v1 whole, which is shorter than its diff:
```python
import functools

import jax
import jax.numpy as jnp
from jax import lax
from jax.experimental import pallas as pl
from jax.experimental.pallas import tpu as pltpu
from jax.sharding import PartitionSpec as P

PASSES = 4
CORES = 2
HI = lax.Precision.HIGHEST
F32 = jnp.float32
BF16 = jnp.bfloat16
MESH = pl.DeviceIdType.MESH


def nt(x, y):
    return lax.dot_general(x, y, (((1,), (1,)), ((), ())), precision=HI, preferred_element_type=F32)


def far_first(offsets, sizes):
    def hops(o):
        return sum(min(d, n - d) for d, n in zip(o, sizes))

    return sorted(offsets, key=lambda o: (-hops(o), o))


def remote(src, dst, send, recv, device):
    return pltpu.make_async_remote_copy(
        src_ref=src, dst_ref=dst, send_sem=send, recv_sem=recv, device_id=device, device_id_type=MESH
    )


def kernel(
    sizes,
    frames,
    a_start,
    b_start,
    c_start,
    a_out,
    b_out,
    c_out,
    a_buf,
    b_buf,
    part_a,
    local_a,
    local_b,
    shared,
    ra,
    za,
    rb,
    yb,
    yzc,
    cg,
    ga,
    gb,
    h_ref,
    gram_c_ref,
    gram_b_ref,
    low_a,
    low_b,
    s_ra,
    s_za,
    s_aa,
    s_ga,
    s_rb,
    s_yb,
    s_ab,
    s_gb,
    s_yzc,
    s_cg,
):
    npx, npy, nfr = sizes
    nx = nfr // CORES
    y, z, fr = lax.axis_index("px"), lax.axis_index("py"), lax.axis_index("fr")
    x, core = fr // CORES, lax.rem(fr, CORES)
    lead, helper = core == 1, core == 0
    rank = a_start.shape[0]
    kk = c_start.shape[0]
    rows = rank // nx
    own = pl.ds(pl.multiple_of(x * rows, rows), rows)
    yz = y * npy + z

    def block(i):
        return pl.ds(pl.multiple_of(i * rows, rows), rows)

    def to_x(d):
        return lax.rem(x + d, nx)

    def from_x(d):
        return lax.rem(x + nx - d, nx)

    x_away = [d for d, in far_first([(d,) for d in range(1, nx)], (nx,))]
    y_away = [d for d, in far_first([(d,) for d in range(1, npx)], (npx,))]
    z_away = [d for d, in far_first([(d,) for d in range(1, npy)], (npy,))]
    yz_away = far_first(
        [(i, j) for i in range(npx) for j in range(npy) if i or j], (npx, npy)
    )

    class Transfers:
        def __init__(self, pairs):
            self.pairs = pairs

        def each(self, act):
            for when, c in self.pairs:
                if when is None:
                    act(c)
                else:
                    pl.when(when)(functools.partial(act, c))

        def start(self):
            self.each(lambda c: c.start())
            return self

        def sent(self):
            self.each(lambda c: c.wait_send())

        def arrived(self):
            self.each(lambda c: c.wait_recv())

    def to_owner(src, dst, sems):
        out = []
        for d in x_away + [0]:
            c = remote(
                src.at[block(to_x(d))],
                dst.at[fr],
                sems.at[0, d],
                sems.at[1, CORES * d + core],
                {"fr": CORES * to_x(d) + 1},
            )
            out.append((None if d else helper, c))
        return Transfers(out).start()

    def at_owner(dst, sems):
        out = []
        for d in [0] + x_away[::-1]:
            for s in (1, 0) if d else (0,):
                slot = dst.at[CORES * from_x(d) + s]
                out.append((None, remote(slot, slot, sems.at[0, 0], sems.at[1, CORES * d + s], {"fr": fr})))
        Transfers(out).arrived()

    def from_owner(buf, sems):
        out = []
        for d in x_away + [0]:
            for s in (0, 1) if d else (0,):
                out.append(
                    (
                        None,
                        remote(
                            buf.at[own],
                            buf.at[own],
                            sems.at[0, CORES * d + s],
                            sems.at[1, d],
                            {"fr": CORES * to_x(d) + s},
                        ),
                    )
                )
        return Transfers(out)

    def at_all(buf, sems):
        out = []
        for d in [0] + x_away[::-1]:
            slot = buf.at[block(from_x(d))]
            out.append((None if d else helper, remote(slot, slot, sems.at[0, 0], sems.at[1, d], {"fr": fr})))
        Transfers(out).arrived()

    def along(axis, me, n, away, dst, sems):
        def copy(d, slot):
            return remote(dst.at[slot], dst.at[slot], sems.at[0, d], sems.at[1, d], {axis: lax.rem(me + d, n)})

        out = Transfers([(None, copy(d, me)) for d in away])
        back = Transfers([(None, copy(d, lax.rem(me + n - d, n))) for d in away[::-1]])
        return out, back

    y_line = functools.partial(along, "px", y, npx, y_away)
    z_line = functools.partial(along, "py", z, npy, z_away)

    def plane(dst, sems):
        def copy(o, slot):
            k = o[0] * npy + o[1]
            there = {"px": lax.rem(y + o[0], npx), "py": lax.rem(z + o[1], npy)}
            return remote(dst.at[slot], dst.at[slot], sems.at[0, k], sems.at[1, k], there)

        def source(o):
            return lax.rem(y + npx - o[0], npx) * npy + lax.rem(z + npy - o[1], npy)

        out = Transfers([(None, copy(o, yz)) for o in yz_away])
        back = Transfers([(None, copy(o, source(o))) for o in yz_away[::-1]])
        return out, back

    barrier = pltpu.get_barrier_semaphore()
    for d in range(1, nfr):
        pl.semaphore_signal(barrier, inc=1, device_id={"fr": lax.rem(fr + d, nfr)}, device_id_type=MESH)
    for i, j in yz_away:
        there = {"px": lax.rem(y + i, npx), "py": lax.rem(z + j, npy)}
        pl.semaphore_signal(barrier, inc=1, device_id=there, device_id_type=MESH)

    eye = lax.broadcasted_iota(jnp.int32, (rank, rank), 0) == lax.broadcasted_iota(
        jnp.int32, (rank, rank), 1
    )

    def turned(column):
        return jnp.sum(jnp.where(eye, column, 0.0), axis=0, keepdims=True)

    def columns_of(c):
        return [
            jnp.sum(jnp.where(eye, c[k : k + 1, :], 0.0), axis=1, keepdims=True) for k in range(kk)
        ]

    def tile_of(c):
        low = jnp.concatenate([c, jnp.zeros((8 - kk, rank), F32)], axis=0)
        return jnp.concatenate([low, jnp.zeros((8, 128 - rank), F32)], axis=1)

    def packed(gram):
        return jnp.concatenate([gram[: rank // 2], gram[rank // 2 :]], axis=1)

    def unpacked(pack):
        return jnp.concatenate([pack[:, :rank], pack[:, rank:]], axis=0)

    def total(ref, n):
        out = ref[0]
        for s in range(1, n):
            out = out + ref[s]
        return out

    def multiply_a(b):
        b_half = b.astype(BF16)
        for k in range(kk):
            part_a[k] = lax.dot_general(
                b_half, frames[k], (((1,), (1,)), ((), ())), preferred_element_type=F32
            )

    a_buf[0] = a_start[...]
    b_buf[0] = b_start[...]
    c = c_start[...]
    c_cols = columns_of(c)
    cg[fr] = tile_of(c)

    to_lead, at_lead = [], []
    for d in x_away + [0]:
        to_lead.append(
            (
                None if d else helper,
                remote(
                    cg.at[fr], cg.at[fr], s_cg.at[0, d], s_cg.at[1, CORES * d + core], {"fr": CORES * to_x(d) + 1}
                ),
            )
        )
    c_send = Transfers(to_lead)
    gb_send, gb_back = z_line(gb, s_gb)
    za_send, za_back = z_line(za, s_za)
    ga_send, ga_back = y_line(ga, s_ga)
    yb_send, yb_back = y_line(yb, s_yb)
    yzc_send, yzc_back = plane(yzc, s_yzc)

    @pl.when(lead)
    def _():
        gb[z] = packed(nt(b_start[...], b_start[...]))

    pl.semaphore_wait(barrier, nfr - 1 + len(yz_away))
    @pl.when(lead)
    def _():
        gb_send.start()

    c_send.start()
    multiply_a(b_start[...])

    for step in range(PASSES):
        now, new = step % 2, (step + 1) % 2
        out = c_cols[0] * part_a[0]
        for k in range(1, kk):
            out = out + c_cols[k] * part_a[k]
        local_a[...] = out
        ra_send = to_owner(local_a, ra, s_ra)

        @pl.when(lead)
        def _():
            at_owner(cg, s_cg)
            if step == 0:
                gb_back.arrived()
                gb_send.sent()
                gram_b_ref[...] = unpacked(total(gb, npy))
            every_c = cg[...].reshape(nfr * 8, 128)
            gram_c = lax.dot_general(
                every_c, every_c, (((0,), (0,)), ((), ())), precision=HI, preferred_element_type=F32
            )[:rank, :rank]
            gram_c_ref[...] = gram_c
            h_ref[...] = gram_b_ref[...] * gram_c
            low_a[...] = jnp.dot(h_ref[own, :], a_buf[now], precision=HI, preferred_element_type=F32)
            ra[fr] = local_a[own, :]
            at_owner(ra, s_ra)
            za[z] = total(ra, nfr)
            za_send.start()

        c_send.sent()
        ra_send.sent()

        @pl.when(lead)
        def _():
            za_back.arrived()
            a_buf[new, own, :] = a_buf[now, own, :] * total(za, npy) / low_a[...]
            from_owner(a_buf.at[new], s_aa).start()
            za_send.sent()

        at_all(a_buf.at[new], s_aa)

        a_half = a_buf[new].astype(BF16)
        out = None
        for k in range(kk):
            part = jnp.dot(a_half, frames[k], preferred_element_type=F32)
            shared[k] = part
            out = c_cols[k] * part if out is None else out + c_cols[k] * part
        local_b[...] = out
        rb_send = to_owner(local_b, rb, s_rb)
        ga[y] = packed(nt(a_buf[new], a_buf[new]))
        ga_send.start()

        @pl.when(lead)
        def _():
            rb[fr] = local_b[own, :]
            at_owner(rb, s_rb)
            yb[y] = total(rb, nfr)
            yb_send.start()

        ga_back.arrived()
        gram_a = unpacked(total(ga, npx))

        @pl.when(lead)
        def _():
            h_ref[...] = gram_a * gram_c_ref[...]
            low_b[...] = jnp.dot(h_ref[own, :], b_buf[now], precision=HI, preferred_element_type=F32)
            yb_back.arrived()
            b_buf[new, own, :] = b_buf[now, own, :] * total(yb, npx) / low_b[...]
            from_owner(b_buf.at[new], s_ab).start()
            yb_send.sent()
            from_owner(a_buf.at[new], s_aa).sent()

        rb_send.sent()
        ga_send.sent()
        at_all(b_buf.at[new], s_ab)

        b_new = b_buf[new]
        rows_c = [turned(jnp.sum(shared[k] * b_new, axis=1, keepdims=True)) for k in range(kk)]
        yzc[yz] = jnp.concatenate(
            [jnp.concatenate(rows_c[k : k + 2], axis=1) for k in range(0, kk, 2)], axis=0
        )
        yzc_send.start()
        gb[z] = packed(nt(b_new, b_new))
        gb_send.start()
        if step + 1 < PASSES:
            multiply_a(b_new)

        @pl.when(lead)
        def _():
            from_owner(b_buf.at[new], s_ab).sent()

        gb_back.arrived()
        gram_b = unpacked(total(gb, npy))
        gram_b_ref[...] = gram_b
        lower = jnp.dot(c, gram_a * gram_b, precision=HI, preferred_element_type=F32)
        yzc_back.arrived()
        pairs = total(yzc, npx * npy)
        m = jnp.concatenate(
            [pairs[k // 2 : k // 2 + 1, k % 2 * rank : (k % 2 + 1) * rank] for k in range(kk)], axis=0
        )
        c = c * m / lower
        yzc_send.sent()
        gb_send.sent()
        if step + 1 < PASSES:
            cg[fr] = tile_of(c)
            c_send.start()
            c_cols = columns_of(c)
    a_out[...] = a_buf[PASSES % 2]
    b_out[...] = b_buf[PASSES % 2]
    c_out[...] = c


def body(sizes, frames, a_start, b_start, c_start):
    npx, npy, nfr = sizes
    nx = nfr // CORES
    rank, i_len = a_start.shape
    j_len = b_start.shape[1]
    kk = c_start.shape[1]
    rows = rank // nx
    vmem = pl.BlockSpec(memory_space=pltpu.VMEM)

    def sems(n):
        return pltpu.SemaphoreType.DMA((2, n))

    a, b, c = pl.pallas_call(
        functools.partial(kernel, sizes),
        name="cp",
        out_shape=[
            jax.ShapeDtypeStruct((rank, i_len), F32),
            jax.ShapeDtypeStruct((rank, j_len), F32),
            jax.ShapeDtypeStruct((kk, rank), F32),
        ],
        in_specs=[vmem] * 4,
        out_specs=[vmem] * 3,
        scratch_shapes=[
            pltpu.VMEM((2, rank, i_len), F32),
            pltpu.VMEM((2, rank, j_len), F32),
            pltpu.VMEM((kk, rank, i_len), F32),
            pltpu.VMEM((rank, i_len), F32),
            pltpu.VMEM((rank, j_len), F32),
            pltpu.VMEM((kk, rank, j_len), F32),
            pltpu.VMEM((nfr, rows, i_len), F32),
            pltpu.VMEM((npy, rows, i_len), F32),
            pltpu.VMEM((nfr, rows, j_len), F32),
            pltpu.VMEM((npx, rows, j_len), F32),
            pltpu.VMEM((npx * npy, kk // 2, 2 * rank), F32),
            pltpu.VMEM((nfr, 8, 128), F32),
            pltpu.VMEM((npx, rank // 2, 2 * rank), F32),
            pltpu.VMEM((npy, rank // 2, 2 * rank), F32),
            pltpu.VMEM((rank, rank), F32),
            pltpu.VMEM((rank, rank), F32),
            pltpu.VMEM((rank, rank), F32),
            pltpu.VMEM((rows, i_len), F32),
            pltpu.VMEM((rows, j_len), F32),
            sems(nfr),
            sems(npy),
            sems(nfr),
            sems(npx),
            sems(nfr),
            sems(npx),
            sems(nfr),
            sems(npy),
            sems(npx * npy),
            sems(nfr),
        ],
        compiler_params=pltpu.CompilerParams(collective_id=0, has_side_effects=True),
    )(frames, a_start, b_start, c_start.T)
    return a, b, c.T


def solution(mesh):
    sizes = (mesh.shape["px"], mesh.shape["py"], mesh.shape["fr"])
    return jax.shard_map(
        functools.partial(body, sizes),
        mesh=mesh,
        in_specs=(P("fr", "px", "py"), P(None, "px"), P(None, "py"), P(None, "fr")),
        out_specs=(P(None, "px"), P(None, "py"), P(None, "fr")),
        check_vma=False,
    )
```

time: 148 us -> 134 us (0.905)
  Pallas kernels: 142 us -> 130 us
  local copies, waits for them, and re-layouts: 5.03 us -> 2.85 us
    pallas_call x1, Pallas kernels: 142 us -> 130 us  [body(): pl.pallas_call(functools.partial(kernel, sizes), name='cp', out_shape=[ja...]
    unnamed x5 -> x7, local copies, waits for them, and re-layouts: 3.62 us -> 2.85 us
where the time goes in v1:
time: 134 us
  Pallas kernels  130 us (97%)
  local copies, waits for them, and re-layouts  2.85 us (2%)
    pallas_call x1, Pallas kernels, body(): pl.pallas_call(functools.partial(kernel, sizes), name='cp', out_shape=[ja...  130 us
    unnamed x7, local copies, waits for them, and re-layouts  2.85 us

profile of v1, /device:TPU:1, one launch (start us, length us, event | category | flops | bytes accessed | tf_op | source)
XLA Modules:
  0.0 133.6 jit_solution(16414108920841487222)
XLA Ops:
  0.6 130.1 %cp.1 = (f32[64,512]{1,0:T(8,128)}, f32[64,256]{1,0:T(8,128)}, f32[4,64]{1,0:T(4,128)}) custom-call(bf16[4,512,256]{2,1,0:T(8,128)(2,1)} %frames.1, f32[64,512]{1,0:T(8,128)} %a_start.1, f32[64,256]{1,0:T(8,128)} %b_start.1, f32[4,64]{1,0:T(4,128)} %bitcast.2), custom_call_target="tpu_custom_call" | custom-call | tf_op jit(solution)/shard_map/cp/pallas_call | solution.py:391
  130.7 0.0 copy-start
  130.8 1.6 %copy.10 = f32[64,512]{1,0:T(8,128)} copy(f32[64,512]{1,0:T(8,128)} %get-tuple-element.12) | data formatting | bytes 262144
  132.4 0.0 copy-done
  132.4 0.0 copy-start.1
  132.4 0.6 copy.11
  133.0 0.0 copy-done.1
  133.0 0.6 copy.12
Async XLA Ops:
  130.7 1.6 %copy-start = (f32[64,256]{1,0:T(8,128)S(1)}, f32[64,256]{1,0:T(8,128)}, u32[]{:S(2)}) copy-start(f32[64,256]{1,0:T(8,128)} %get-tuple-element.13) | copy-start | bytes 196612
  132.4 0.7 copy-start.1
